TPU v7x, 256 devices: a whole 4x4x8 slice. The times are simulated.
256 devices in a mesh: seq: 8 (over z), chan: 32 (over y, x, core).
Axes of the slice: x: 4, y: 4, z: 8, core: 2. Of those that a mesh axis runs over, the one named last changes fastest.
Arguments:
- tokens: bfloat16 [8192, 4096], P('seq', 'chan'), may hold values from -8 to 8
- norm_gain: float32 [4096], replicated, may hold values from 0.5 to 1.5
- gate_proj: bfloat16 [4096, 8192], P(None, 'chan'), may hold values from -0.09375 to 0.09375
- inner_proj: bfloat16 [4096, 8192], P(None, 'chan'), may hold values from -0.09375 to 0.09375
- state_proj: bfloat16 [4096, 384], P('chan'), may hold values from -0.11816406 to 0.11816406
- conv_inner: float32 [4, 8192], P(None, 'chan'), may hold values from -3 to 3
- conv_state: float32 [4, 256], replicated, may hold values from -3 to 3
- log_rate: float32 [128], P('chan'), may hold values from -1 to 0
- rate_bias: float32 [128], P('chan'), may hold values from -16 to -2
- skip_gain: float32 [128], P('chan'), may hold values from 0.2 to 4
- gate_gain: float32 [8192], P('chan'), may hold values from 0.5 to 1.5
- out_proj: bfloat16 [8192, 4096], P('chan'), may hold values from -0.125 to 0.125
Outputs:
- layer_out: bfloat16 [8192, 4096], P('seq', 'chan')
All inputs are finite; a program needn't handle non-finite values.
Results may differ from a plain program's by a relative error of at most 0.012.
Values may be sent and summed in bfloat16 or wider, within the bound.
A program may use at most 128 MiB of HBM per device.

v0:
```python
import jax
import jax.numpy as jnp
from jax import lax
from jax.sharding import PartitionSpec as P

P_SIZE = 64
N = 128
K = 4
Q = 256
DI = 8192


def from_behind(value, axis, steps):
    count = lax.axis_size(axis)
    leading, last = (max(0, -steps), min(count, count - steps))
    return lax.ppermute(value, axis, [(source, source + steps) for source in range(leading, last)])


def prefix(value, axis, join, neutral):
    count, mine = (lax.axis_size(axis), lax.axis_index(axis))
    pieces = jax.tree.map(lambda part: lax.all_gather(part, axis), value)
    total = jax.tree.map(
        lambda part, zero: jnp.full_like(part, 0) + jnp.asarray(zero, part.dtype), value, neutral
    )

    def turn(position, total):
        longer = join(total, jax.tree.map(lambda part: part[position], pieces))
        return jax.tree.map(lambda new, old: jnp.where(position < mine, new, old), longer, total)

    return lax.fori_loop(0, count - 1, turn, total)


def from_everyone(x, axis):
    size = lax.axis_size(axis)
    return lax.all_to_all(jnp.broadcast_to(x[None], (size, *x.shape)), axis, 0, 0, tiled=True)


def over_copies(x, axis):
    everything = from_everyone(x, axis)
    return jnp.sum(everything, axis=0)


def causal_mix(rim_part, fresh_rows, weights):
    length = fresh_rows.shape[0]
    padded = jnp.concatenate([rim_part.astype(jnp.float32), fresh_rows.astype(jnp.float32)], axis=0)
    summed = jnp.zeros(fresh_rows.shape, jnp.float32)
    for offset in range(weights.shape[0]):
        summed = summed + weights[offset] * padded[offset : offset + length]
    return jax.nn.silu(summed)


def combine_pair(earlier_part, later_part):
    return (
        earlier_part[0] * later_part[0],
        later_part[0][:, None, None] * earlier_part[1] + later_part[1],
    )


def local(
    tokens,
    norm_gain,
    gate_proj,
    inner_proj,
    state_proj,
    conv_inner,
    conv_state,
    log_rate,
    rate_bias,
    skip_gain,
    gate_gain,
    out_proj,
):
    gathered = lax.all_gather(tokens, "chan", axis=1, tiled=True)
    widened = gathered.astype(jnp.float32)
    inverse = lax.rsqrt(jnp.mean(widened * widened, axis=1, keepdims=True) + 1e-05)
    normed = (widened * inverse * norm_gain).astype(jnp.bfloat16)
    gate_raw = jnp.dot(normed, gate_proj, preferred_element_type=jnp.float32).astype(jnp.bfloat16)
    inner_raw = jnp.dot(normed, inner_proj, preferred_element_type=jnp.float32).astype(jnp.bfloat16)
    heads = log_rate.shape[0]
    start_head = lax.axis_index("chan") * heads
    projected = jnp.dot(
        normed,
        lax.all_gather(state_proj, "chan", axis=0, tiled=True),
        preferred_element_type=jnp.float32,
    )
    state_raw = projected[:, : 2 * N]
    raw_rate = lax.dynamic_slice_in_dim(projected, 2 * N + start_head, heads, 1)
    rim_rows = from_behind(
        (inner_raw[-(K - 1) :].astype(jnp.float32), state_raw[-(K - 1) :]), "seq", 1
    )
    inner_conv = causal_mix(rim_rows[0].astype(jnp.bfloat16), inner_raw, conv_inner)
    state_conv = causal_mix(rim_rows[1], state_raw, conv_state)
    token_rows = tokens.shape[0]
    blocks = token_rows // Q
    step_size = jax.nn.softplus(raw_rate + rate_bias)
    decay_log = -jnp.exp(log_rate) * step_size
    values = inner_conv.reshape(blocks, Q, heads, P_SIZE)
    in_map = state_conv[:, :N].reshape(blocks, Q, N)
    out_map = state_conv[:, N:].reshape(blocks, Q, N)
    step_rows = step_size.reshape(blocks, Q, heads).transpose(0, 2, 1)
    log_rows = decay_log.reshape(blocks, Q, heads).transpose(0, 2, 1)
    lower_mask = (jnp.arange(Q)[:, None] >= jnp.arange(Q)[None, :]).astype(jnp.float32)
    within = jnp.einsum("chs,ts->cht", log_rows, lower_mask)
    log_gaps = within[..., :, None] - within[..., None, :]
    fading = jnp.exp(jnp.where(lower_mask > 0, log_gaps, -jnp.inf))
    scores = jnp.einsum("ctn,csn->cts", out_map, in_map)
    mixing = scores[:, None] * fading * step_rows[:, :, None, :]
    local_out = jnp.einsum("chts,cshp->cthp", mixing, values)
    tail_weight = jnp.exp(within[..., -1:] - within) * step_rows
    scaled = values * tail_weight.transpose(0, 2, 1)[..., None]
    block_end = jnp.einsum("csn,cshp->chnp", in_map, scaled)
    block_log = within[..., -1]
    through = jnp.cumsum(block_log, axis=0)
    before = through - block_log
    earlier = jnp.arange(blocks)[:, None] > jnp.arange(blocks)[None, :]
    passage = jnp.exp(
        jnp.where(earlier[:, :, None], before[:, None, :] - through[None, :, :], -jnp.inf)
    )
    entering = jnp.einsum("cdh,dhnp->chnp", passage, block_end)
    device_end = jnp.einsum("ch,chnp->hnp", jnp.exp(through[-1:] - through), block_end)
    device_fade = jnp.exp(through[-1])
    identity = (jnp.ones_like(device_fade), jnp.zeros_like(device_end))
    carried = prefix((device_fade, device_end), "seq", combine_pair, identity)[1]
    entering = entering + jnp.exp(before)[:, :, None, None] * carried[None]
    carried_out = jnp.einsum("ctn,chnp->cthp", out_map, entering)
    carried_out = carried_out * jnp.exp(within).transpose(0, 2, 1)[..., None]
    skip_wide = jnp.repeat(skip_gain, P_SIZE)
    ssd_out = (local_out + carried_out).reshape(token_rows, heads * P_SIZE) + skip_wide * inner_conv
    gated_out = ssd_out * jax.nn.silu(gate_raw.astype(jnp.float32))
    energy = over_copies(jnp.sum(gated_out * gated_out, axis=1), "chan")
    norm_scale = lax.rsqrt(energy / DI + 1e-05)
    shaped = (gated_out * norm_scale[:, None] * gate_gain).astype(jnp.bfloat16)
    column_rows = lax.all_to_all(out_proj, "chan", split_axis=1, concat_axis=0, tiled=True)
    summed = jnp.dot(
        lax.all_gather(shaped, "chan", axis=1, tiled=True),
        column_rows,
        preferred_element_type=jnp.float32,
    )
    return (tokens.astype(jnp.float32) + summed).astype(jnp.bfloat16)


def solution(mesh):
    return jax.shard_map(
        local,
        mesh=mesh,
        in_specs=(
            P("seq", "chan"),
            P(),
            P(None, "chan"),
            P(None, "chan"),
            P("chan", None),
            P(None, "chan"),
            P(),
            P("chan"),
            P("chan"),
            P("chan"),
            P("chan"),
            P("chan", None),
        ),
        out_specs=P("seq", "chan"),
        check_vma=False,
    )
```

profile of v0, /device:TPU:1, one launch (start us, length us, event | category | flops | bytes accessed | tf_op | source)
XLA Modules:
  0.0 364.0 jit_solution(8693260345117643009)
XLA Ops:
  6.5 0.7 all-gather.7.cloned.1.call-update
  7.3 0.7 all-gather.9.cloned.1.call-update
  8.1 0.7 exponential_negate_fusion
  8.7 0.8 fusion.68
  9.6 0.8 fusion.69
  10.4 67.4 %all-gather.7.cloned.1.call-done = bf16[1024,4096]{1,0:T(8,128)(2,1)} async-done(((bf16[1024,128]{1,0:T(8,128)(2,1)}), bf16[1024,4096]{1,0:T(8,128)(2,1)}) %all-gather.7.cloned.1.call-update) | async-done | bytes 8388624 | tf_op jit(solution)/shard_map/all_gather | solution.py:73
  77.8 5.1 %fusion.1 = f32[1024]{0:T(1024)S(1)} fusion(bf16[1024,4096]{1,0:T(8,128)(2,1)} %all-gather.7.cloned.1.call-done), kind=kLoop, calls=%fused_computation.6 | loop fusion | flops 12581888 | bytes 8392704 | tf_op jit(solution)/shard_map/reduce_sum | solution.py:75
  82.9 47.1 %all-gather.9.cloned.1.call-done = bf16[4096,384]{1,0:T(8,128)(2,1)} async-done(((bf16[128,384]{1,0:T(8,128)(2,1)}), bf16[4096,384]{1,0:T(8,128)(2,1)}) %all-gather.9.cloned.1.call-update) | async-done | bytes 3145744 | tf_op jit(solution)/shard_map/all_gather | solution.py:83
  130.0 8.1 %fusion.63 = f32[1024,384]{1,0:T(8,128)S(1)} fusion(bf16[4096,384]{1,0:T(8,128)(2,1)} %all-gather.9.cloned.1.call-done, bf16[1024,4096]{1,0:T(8,128)(2,1)} %all-gather.7.cloned.1.call-done, f32[4096]{0:T(1024)S(1)} %copy-done.10, f32[1024]{0:T(1024)S(1)} %add_rsqrt_fusion.1), kind=kOutput, calls=%fused_computation.97 | convolution fusion | flops 3238002688 | bytes 13127680 | tf_op jit(solution)/shard_map/dot_general | solution.py:81
  138.1 3.2 collective-permute-start.1
  141.3 0.2 constant_dynamic-slice_fusion.1
  141.5 0.2 copy.156
  141.7 0.1 broadcast_multiply_fusion.1
  141.8 0.2 fusion.50
  142.0 0.2 slice_reduce_fusion
  142.3 5.9 %fusion.70 = (f32[1024,256]{1,0:T(8,128)S(1)}, bf16[1024,256]{1,0:T(8,128)(2,1)S(1)}) fusion(bf16[4096,256]{1,0:T(8,128)(2,1)S(1)} %copy-done, bf16[1024,4096]{1,0:T(8,128)(2,1)} %all-gather.7.cloned.1.call-done, f32[4096]{0:T(1024)S(1)} %copy-done.10, f32[1024]{0:T(1024)S(1)} %add_rsqrt_fusion.1), kind=kOutput, calls=%fused_computation.102 | convolution fusion | flops 2164785152 | bytes 12079104 | tf_op jit(solution)/shard_map/dot_general | solution.py:78
  148.2 3.2 collective-permute-start
  151.5 1.1 slice.93
  152.6 0.6 divide_multiply_fusion.1
  153.2 1.3 copy.120
  154.5 2.8 reshape.81
  157.3 1.4 broadcast_multiply_fusion
  158.7 3.1 divide_multiply_fusion
  161.9 0.7 copy-done.5
  162.6 0.9 fusion.47
  164.2 12.4 %all-gather.1 = f32[8,1,4]{2,1,0:T(1,128)S(1)} all-gather(f32[1,1,4]{2,1,0:T(1,128)S(1)} %get-tuple-element.179), channel_id=1, replica_groups=mesh['seq'=8,'chan'=32] {'seq'}, dimensions={0}, use_global_device_ids=true | all-gather | bytes 144 | tf_op jit(solution)/shard_map/all_gather | solution.py:21
  176.6 2.2 fusion.71
  178.8 19.2 %all-gather.13.cloned.1.call-done = f32[32,128,64]{1,2,0:T(8,128)} async-done(((f32[4,128,64]{1,2,0:T(8,128)}), f32[32,128,64]{1,2,0:T(8,128)}) %all-gather.13.cloned.1.call-update) | async-done | bytes 1048592 | tf_op jit(solution)/shard_map/all_gather | solution.py:21
  198.0 8.4 %while.14 = (s32[]{:T(128)}, f32[4,128,64]{2,1,0:T(8,128)S(1)}, s32[]{:T(128)}, f32[8,4]{1,0:T(8,128)S(1)}, f32[8,4,128,64]{2,3,1,0:T(8,128)}, /*index=5*/s32[]{:T(128)}, s32[]{:T(128)}) while((s32[]{:T(128)}, f32[4,128,64]{2,1,0:T(8,128)S(1)}, s32[]{:T(128)}, f32[8,4]{1,0:T(8,128)S(1)}, f32[8,4,128,64]{2,3,1,0:T(8,128)}, ...), condition=%wide.region_3.4_spmd.clone, body=%wide.region_2.3_spmd.clone.sunk | while | flops 131076 | bytes 917665 | solution.py:30
  198.0 0.9 constant_dynamic-slice_fusion.3
  198.9 0.1 copy.166
  199.0 0.1 fusion.85
  199.2 0.9 constant_dynamic-slice_fusion.3
  200.1 0.1 copy.166
  200.2 0.1 fusion.85
  200.4 0.9 constant_dynamic-slice_fusion.3
  201.3 0.1 copy.166
  201.4 0.1 fusion.85
  201.6 0.9 constant_dynamic-slice_fusion.3
  202.5 0.1 copy.166
  202.6 0.1 fusion.85
  202.8 0.9 constant_dynamic-slice_fusion.3
  203.7 0.1 copy.166
  203.8 0.1 fusion.85
  204.0 0.9 constant_dynamic-slice_fusion.3
  204.9 0.1 copy.166
  205.0 0.1 fusion.85
  205.2 0.9 constant_dynamic-slice_fusion.3
  206.1 0.1 copy.166
  206.2 0.1 fusion.85
  206.3 0.1 copy.135
  206.5 0.4 fusion.22
  206.9 0.3 fusion.72
  207.2 3.9 %fusion.19 = f32[4,256,4,64]{1,3,2,0:T(8,128)} fusion(f32[4,4,256]{2,1,0:T(4,128)S(1)} %copy.123, f32[4,4,256]{2,1,0:T(4,128)S(1)} %fusion.50, f32[4,256,256]{2,1,0:T(8,128)} %fusion.71, pred[256,256]{1,0:T(8,128)(4,1)S(1)} %convert_compare_fusion, f32[4,256,4,64]{1,0,3,2:T(4,128)} %reshape.81, f32[4,256,4,64]{1,3,2,0:T(8,128)S(1)} %bitcast.90, ...), kind=kOutput, calls=%fused_computation.26 | convolution fusion | flops 138936320 | bytes 4308992 | tf_op jit(solution)/shard_map/chts,cshp->cthp/dot_general | solution.py:108
  211.1 2.9 copy.152
  213.9 3.2 reshape.97
  217.2 7.8 %multiply_reduce_fusion = (f32[1024]{0:T(1024)S(1)}, f32[1024,256]{1,0:T(8,128)}) fusion(bf16[4096,256]{1,0:T(8,128)(2,1)} %param.16, bf16[1024,4096]{1,0:T(8,128)(2,1)} %all-gather.7.cloned.1.call-done, f32[4096]{0:T(1024)S(1)} %copy-done.10, f32[1024]{0:T(1024)S(1)} %add_rsqrt_fusion.1, f32[1024,256]{1,0:T(8,128)} %reshape.97, ...), kind=kOutput, calls=%fused_computation.61 | convolution fusion | flops 2167143424 | bytes 13657088 | tf_op jit(solution)/shard_map/dot_general | solution.py:77
  225.0 19.9 %all_to_all.25 = f32[32,1,1024]{2,1,0:T(1,128)S(1)} all-to-all(f32[32,1,1024]{2,1,0:T(1,128)S(1)} %broadcast_in_dim.32), channel_id=1, replica_groups=mesh['seq'=8,'chan'=32] {'chan'}, dimensions={0} | all-to-all | bytes 262144 | tf_op jit(solution)/shard_map/all_to_all | solution.py:35
  245.1 2.2 multiply_convert_fusion
  247.4 4.1 %copy.141 = bf16[256,4096]{0,1:T(8,128)(2,1)} copy(bf16[256,4096]{1,0:T(8,128)(2,1)} %param.25) | data formatting | bytes 4194304 | tf_op args[11]
  251.4 39.8 %all_to_all.26 = bf16[256,32,128]{0,2,1:T(8,128)(2,1)} all-to-all(bf16[256,32,128]{0,2,1:T(8,128)(2,1)} %bitcast.86), channel_id=1, replica_groups=mesh['seq'=8,'chan'=32] {'chan'}, dimensions={1} | all-to-all | bytes 4194304 | tf_op jit(solution)/shard_map/all_to_all | solution.py:133
  291.3 4.1 %copy.142 = bf16[32,256,128]{2,1,0:T(8,128)(2,1)} copy(bf16[32,256,128]{1,2,0:T(8,128)(2,1)} %bitcast.85) | data formatting | bytes 4194304 | tf_op jit(solution)/shard_map/all_to_all | solution.py:133
  295.3 50.5 %all-gather.11.cloned.1.call-done = bf16[1024,8192]{1,0:T(8,128)(2,1)} async-done(((bf16[1024,256]{1,0:T(8,128)(2,1)}), bf16[1024,8192]{1,0:T(8,128)(2,1)}) %all-gather.11.cloned.1.call-update) | async-done | bytes 16777232 | tf_op jit(solution)/shard_map/all_gather | solution.py:135
  345.8 11.6 %fusion.23 = bf16[1024,128]{1,0:T(8,128)(2,1)} fusion(bf16[1024,8192]{1,0:T(8,128)(2,1)} %all-gather.11.cloned.1.call-done, bf16[8192,128]{1,0:T(8,128)(2,1)} %bitcast.89, bf16[1024,128]{1,0:T(8,128)(2,1)S(1)} %copy-done.6), kind=kOutput, calls=%fused_computation.34 | convolution fusion | flops 2147876864 | bytes 19398656 | tf_op jit(solution)/shard_map/dot_general | solution.py:134
  (61 shorter events, 1.2 us)
Async XLA Ops:
  6.5 135.8 %copy-start = (bf16[4096,256]{1,0:T(8,128)(2,1)S(1)}, bf16[4096,256]{1,0:T(8,128)(2,1)}, u32[]{:S(2)}) copy-start(bf16[4096,256]{1,0:T(8,128)(2,1)} %param.17) | copy-start | bytes 6291460
  6.5 71.3 %all-gather.7.cloned.1.call-start = ((), (), s32[]{:S(2)}) async-start(), calls=%async_computation.2 | async-start | bytes 8650752 | tf_op jit(solution)/shard_map/all_gather | solution.py:73
  7.3 122.7 %all-gather.9.cloned.1.call-start = ((), (), s32[]{:S(2)}) async-start(), calls=%async_computation.3 | async-start | bytes 3244032 | tf_op jit(solution)/shard_map/all_gather | solution.py:83
  8.0 189.9 %all-gather.13.cloned.1.call-start = ((), (), s32[]{:S(2)}) async-start(), calls=%async_computation.5 | async-start | bytes 1179648 | tf_op jit(solution)/shard_map/all_gather | solution.py:21
  10.4 119.6 %copy-start.10 = (f32[4096]{0:T(1024)S(1)}, f32[4096]{0:T(1024)}, u32[]{:S(2)}) copy-start(f32[4096]{0:T(1024)} %param.15) | copy-start | bytes 49156
  82.9 58.8 %copy-start.8 = (f32[4]{0:T(128)S(1)}, f32[4]{0:T(128)}, u32[]{:S(2)}) copy-start(f32[4]{0:T(128)} %param.22) | copy-start | bytes 52
  138.1 3.2 copy-start.3
  138.1 20.6 %collective-permute-start.1 = (f32[3,256]{1,0:T(4,128)S(1)}, f32[3,256]{1,0:T(4,128)S(1)}, u32[]{:S(2)}, u32[]{:S(2)}) collective-permute-start(f32[3,256]{1,0:T(4,128)S(1)} %slice.92), channel_id=1, source_target_pairs={{0,32},{32,64},{64,96},{96,128},{128,160},{160,192},{192,224},{1,3... | collective-permute-start | bytes 9224 | tf_op jit(solution)/shard_map/ppermute | solution.py:16
  142.3 9.1 %copy-start.4 = (f32[1024,384]{1,0:T(8,128)S(1)}, f32[1024,384]{1,0:T(8,128)}, u32[]{:S(2)}) copy-start(f32[1024,384]{1,0:T(8,128)} %copy-done.3) | copy-start | bytes 4718596
  148.2 4.3 %collective-permute-start = (bf16[3,256]{1,0:T(4,128)(2,1)S(1)}, bf16[3,256]{1,0:T(4,128)(2,1)S(1)}, u32[]{:S(2)}, u32[]{:S(2)}) collective-permute-start(bf16[3,256]{1,0:T(4,128)(2,1)S(1)} %slice.161), channel_id=1, source_target_pairs={{0,32},{32,64},{64,96},{96,128},{128,160},{160,192},{192,224},{1,3... | collective-permute-start | bytes 4616 | tf_op jit(solution)/shard_map/ppermute | solution.py:16
  153.2 8.7 %copy-start.1 = (f32[1024,256]{1,0:T(8,128)}, f32[1024,256]{1,0:T(8,128)S(1)}, u32[]{:S(2)}) copy-start(f32[1024,256]{1,0:T(8,128)S(1)} %divide_multiply_fusion.1) | copy-start | bytes 3145732
  154.5 9.1 %copy-start.9 = (f32[4]{0:T(128)S(1)}, f32[4]{0:T(128)}, u32[]{:S(2)}) copy-start(f32[4]{0:T(128)} %param.23) | copy-start | bytes 52
  161.9 0.7 copy-start.5
  163.6 182.2 %all-gather.11.cloned.1.call-start = ((), (), s32[]{:S(2)}) async-start(), calls=%async_computation.4 | async-start | bytes 17301504 | tf_op jit(solution)/shard_map/all_gather | solution.py:135
  211.1 6.1 %copy-start.2 = (f32[1024,256]{1,0:T(8,128)S(1)}, f32[1024,256]{1,0:T(8,128)}, u32[]{:S(2)}) copy-start(f32[1024,256]{1,0:T(8,128)} %copy-done.1) | copy-start | bytes 3145732
  217.2 27.9 %copy-start.7 = (f32[256]{0:T(256)S(1)}, f32[256]{0:T(256)}, u32[]{:S(2)}) copy-start(f32[256]{0:T(256)} %param.24) | copy-start | bytes 3076
  251.4 94.4 %copy-start.6 = (bf16[1024,128]{1,0:T(8,128)(2,1)S(1)}, bf16[1024,128]{1,0:T(8,128)(2,1)}, u32[]{:S(2)}) copy-start(bf16[1024,128]{1,0:T(8,128)(2,1)} %param.14) | copy-start | bytes 786436
Sparse Core Ops, SparseCore 0:
  9.8 67.9 all-gather.6
  80.4 49.5 all-gather.8
  163.7 34.1 all-gather.12
  247.5 98.2 all-gather.10
where the time goes:
time: 365 us; the launch traced here: 364 us
  waiting for transfers between devices  186 us (51%)
  blocking collectives  72.1 us (20%)
  matrix products  41.3 us (11%)
  local copies, waits for them, and re-layouts  30.5 us (8%)
  other arithmetic  14.3 us (4%)
  between operations  13.4 us (4%)
  starting transfers between devices  6.52 us (2%)
    all_gather x1, waiting for transfers between devices, local(): gathered = lax.all_gather(tokens, 'chan', axis=1, tiled=True)  67.4 us
    all_gather x1, waiting for transfers between devices, local(): lax.all_gather(shaped, 'chan', axis=1, tiled=True)  50.5 us
    all_gather x1, waiting for transfers between devices, local(): lax.all_gather(state_proj, 'chan', axis=0, tiled=True)  47.1 us
    all_to_all x1, blocking collectives, local(): lax.all_to_all(out_proj, 'chan', split_axis=1, concat_axis=0, tiled=True)  39.8 us
    all_to_all x1, blocking collectives, from_everyone(): lax.all_to_all(jnp.broadcast_to(x[None], (size, *x.shape)), axis, 0, 0, t...  19.9 us
    all_gather x1, waiting for transfers between devices, prefix(): pieces = jax.tree.map(lambda part: lax.all_gather(part, axis), value)  19.2 us
    all_gather x1, blocking collectives, prefix(): pieces = jax.tree.map(lambda part: lax.all_gather(part, axis), value)  12.4 us
    dot_general x1, matrix products, local(): jnp.dot(lax.all_gather(shaped, 'chan', axis=1, tiled=True), column_rows,...  11.6 us
  transfers between devices with their start and end apart: 6, of which 4 were waited for; matrix products, arithmetic and copies ran while one was open for 9% of the time, Pallas kernels for 0%

commit v1 on v0

--- a/solution.py
+++ b/solution.py
@@ -70,7 +70,8 @@
     gate_gain,
     out_proj,
 ):
-    gathered = lax.all_gather(tokens, "chan", axis=1, tiled=True)
+    parts = lax.all_gather(tokens, "chan")
+    gathered = jnp.concatenate(parts, axis=1)
     widened = gathered.astype(jnp.float32)
     inverse = lax.rsqrt(jnp.mean(widened * widened, axis=1, keepdims=True) + 1e-05)
     normed = (widened * inverse * norm_gain).astype(jnp.bfloat16)

time: 365 us -> 349 us (0.956)
  waiting for transfers between devices: 186 us -> 144 us
  other arithmetic: 14.3 us -> 31 us
  local copies, waits for them, and re-layouts: 30.5 us -> 40.3 us
    all_gather x1, waiting for transfers between devices: 47.1 us -> 9.05 us  [local(): lax.all_gather(state_proj, 'chan', axis=0, tiled=True)]
    convert_element_type x0 -> x2, other arithmetic: none -> 20.4 us  [the longest x1 11.1 us: local(): widened = gathered.astype(jnp.float32)]
    convert_element_type x0 -> x1, local copies, waits for them, and re-layouts: none -> 17.5 us  [local(): widened = gathered.astype(jnp.float32)]
    all_gather x1, waiting for transfers between devices: 67.4 us -> 61.5 us  [local(): parts = lax.all_gather(tokens, 'chan')]
  transfers between devices with their start and end apart: 6 -> 6, of which waited for: 4 -> 5; matrix products, arithmetic and copies ran while one was open for 9% -> 18% of each run, Pallas kernels for 0% -> 0%
where the time goes in v1:
time: 349 us
  waiting for transfers between devices  144 us (41%)
  blocking collectives  73.7 us (21%)
  local copies, waits for them, and re-layouts  40.3 us (12%)
  matrix products  39.8 us (11%)
  other arithmetic  31 us (9%)
  between operations  13.4 us (4%)
  starting transfers between devices  6.48 us (2%)
    all_gather x1, waiting for transfers between devices, local(): parts = lax.all_gather(tokens, 'chan')  61.5 us
    all_gather x1, waiting for transfers between devices, local(): lax.all_gather(shaped, 'chan', axis=1, tiled=True)  50.9 us
    all_to_all x1, blocking collectives, local(): lax.all_to_all(out_proj, 'chan', split_axis=1, concat_axis=0, tiled=True)  41 us
    all_gather x1, waiting for transfers between devices, prefix(): pieces = jax.tree.map(lambda part: lax.all_gather(part, axis), value)  20.1 us
    all_to_all x1, blocking collectives, from_everyone(): lax.all_to_all(jnp.broadcast_to(x[None], (size, *x.shape)), axis, 0, 0, t...  19.9 us
    convert_element_type x1, local copies, waits for them, and re-layouts, local(): widened = gathered.astype(jnp.float32)  17.5 us
    all_gather x1, blocking collectives, prefix(): pieces = jax.tree.map(lambda part: lax.all_gather(part, axis), value)  12.8 us
    dot_general x1, matrix products, local(): jnp.dot(lax.all_gather(shaped, 'chan', axis=1, tiled=True), column_rows,...  11.8 us
  transfers between devices with their start and end apart: 6, of which 5 were waited for; matrix products, arithmetic and copies ran while one was open for 18% of the time, Pallas kernels for 0%

profile of v1, /device:TPU:1, one launch (start us, length us, event | category | flops | bytes accessed | tf_op | source)
XLA Modules:
  0.0 348.5 jit_solution(4467841990259172250)
XLA Ops:
  6.5 0.7 all-gather.12.cloned.1.call-update
  7.3 0.7 all-gather.8.cloned.1.call-update
  8.1 0.7 exponential_negate_fusion
  8.7 0.8 fusion.64
  9.6 0.8 fusion.65
  10.4 61.5 %all-gather.12.cloned.1.call-done = bf16[32768,128]{1,0:T(8,128)(2,1)} async-done(((bf16[1024,128]{1,0:T(8,128)(2,1)}), bf16[32768,128]{1,0:T(8,128)(2,1)}) %all-gather.12.cloned.1.call-update) | async-done | bytes 8388624 | tf_op jit(solution)/shard_map/all_gather | solution.py:73
  71.9 11.1 %convert_bitcast_fusion = f32[1024,32,128]{2,0,1:T(8,128)} fusion(bf16[32768,128]{1,0:T(8,128)(2,1)} %all-gather.12.cloned.1.call-done), kind=kLoop, calls=%fused_computation.5 | loop fusion | flops 4194304 | bytes 25165824 | tf_op jit(solution)/shard_map/convert_element_type | solution.py:75
  83.0 17.5 %copy.124 = f32[1024,32,128]{0,2,1:T(8,128)} copy(f32[1024,32,128]{2,0,1:T(8,128)} %convert_bitcast_fusion) | data formatting | bytes 33554432 | tf_op jit(solution)/shard_map/convert_element_type | solution.py:75
  100.5 5.1 %fusion.1 = f32[1024]{0:T(1024)S(1)} fusion(bf16[32,1024,128]{2,1,0:T(8,128)(2,1)} %bitcast.99), kind=kLoop, calls=%fused_computation.6 | loop fusion | flops 12581888 | bytes 8392704 | tf_op jit(solution)/shard_map/reduce_sum | solution.py:76
  105.6 9.3 %fusion.3 = bf16[1024,4096]{0,1:T(8,128)(2,1)} fusion(f32[1024,32,128]{0,2,1:T(8,128)} %copy.124, f32[4096]{0:T(1024)S(1)} %copy-done.5, f32[1024]{0:T(1024)S(1)} %add_rsqrt_fusion.1), kind=kLoop, calls=%fused_computation.9 | loop fusion | flops 12582912 | bytes 25186304 | tf_op jit(solution)/shard_map/convert_element_type | solution.py:77
  114.9 9.0 %all-gather.8.cloned.1.call-done = bf16[4096,384]{1,0:T(8,128)(2,1)} async-done(((bf16[128,384]{1,0:T(8,128)(2,1)}), bf16[4096,384]{1,0:T(8,128)(2,1)}) %all-gather.8.cloned.1.call-update) | async-done | bytes 3145744 | tf_op jit(solution)/shard_map/all_gather | solution.py:84
  123.9 7.9 %fusion.67 = f32[1024,384]{1,0:T(8,128)S(1)} fusion(bf16[1024,4096]{0,1:T(8,128)(2,1)} %fusion.3, bf16[4096,384]{1,0:T(8,128)(2,1)} %all-gather.8.cloned.1.call-done), kind=kOutput, calls=%fused_computation.103 | convolution fusion | flops 3221225472 | bytes 13107200 | tf_op jit(solution)/shard_map/dot_general | solution.py:82
  131.9 3.2 collective-permute-start.1
  135.1 0.2 constant_dynamic-slice_fusion.1
  135.3 0.2 copy.161
  135.5 0.1 broadcast_multiply_fusion.1
  135.6 0.2 fusion.50
  135.7 0.2 slice_reduce_fusion
  136.1 5.7 %fusion.66 = (f32[1024,256]{1,0:T(8,128)S(1)}, bf16[1024,256]{1,0:T(8,128)(2,1)S(1)}) fusion(bf16[1024,4096]{0,1:T(8,128)(2,1)} %fusion.3, bf16[4096,256]{1,0:T(8,128)(2,1)S(1)} %copy-done), kind=kOutput, calls=%fused_computation.102 | convolution fusion | flops 2148007936 | bytes 12058624 | tf_op jit(solution)/shard_map/dot_general | solution.py:79
  141.8 3.2 collective-permute-start
  145.1 0.7 collective-permute-done
  145.8 0.6 divide_multiply_fusion.1
  146.4 1.3 copy.125
  147.7 1.7 reshape.85
  149.4 0.2 broadcast_multiply_fusion
  149.6 0.6 divide_multiply_fusion
  150.3 0.9 fusion.47
  151.9 12.8 %all-gather.2 = f32[8,1,4]{2,1,0:T(1,128)S(1)} all-gather(f32[1,1,4]{2,1,0:T(1,128)S(1)} %get-tuple-element.179), channel_id=1, replica_groups=mesh['seq'=8,'chan'=32] {'seq'}, dimensions={0}, use_global_device_ids=true | all-gather | bytes 144 | tf_op jit(solution)/shard_map/all_gather | solution.py:21
  164.7 1.3 fusion.68
  166.0 20.1 %all-gather.14.cloned.1.call-done = f32[32,128,64]{1,2,0:T(8,128)} async-done(((f32[4,128,64]{1,2,0:T(8,128)}), f32[32,128,64]{1,2,0:T(8,128)}) %all-gather.14.cloned.1.call-update) | async-done | bytes 1048592 | tf_op jit(solution)/shard_map/all_gather | solution.py:21
  186.1 8.4 %while.14 = (s32[]{:T(128)}, f32[4,128,64]{2,1,0:T(8,128)S(1)}, s32[]{:T(128)}, f32[8,4]{1,0:T(8,128)S(1)}, f32[8,4,128,64]{2,3,1,0:T(8,128)}, /*index=5*/s32[]{:T(128)}, s32[]{:T(128)}) while((s32[]{:T(128)}, f32[4,128,64]{2,1,0:T(8,128)S(1)}, s32[]{:T(128)}, f32[8,4]{1,0:T(8,128)S(1)}, f32[8,4,128,64]{2,3,1,0:T(8,128)}, ...), condition=%wide.region_3.4_spmd.clone, body=%wide.region_2.3_spmd.clone.sunk | while | flops 131076 | bytes 917665 | solution.py:30
  186.1 0.9 constant_dynamic-slice_fusion.3
  187.0 0.1 copy.171
  187.1 0.1 fusion.85
  187.3 0.9 constant_dynamic-slice_fusion.3
  188.2 0.1 copy.171
  188.3 0.1 fusion.85
  188.5 0.9 constant_dynamic-slice_fusion.3
  189.4 0.1 copy.171
  189.5 0.1 fusion.85
  189.7 0.9 constant_dynamic-slice_fusion.3
  190.6 0.1 copy.171
  190.7 0.1 fusion.85
  190.9 0.9 constant_dynamic-slice_fusion.3
  191.8 0.1 copy.171
  191.9 0.1 fusion.85
  192.1 0.9 constant_dynamic-slice_fusion.3
  193.0 0.1 copy.171
  193.3 0.9 constant_dynamic-slice_fusion.3
  194.2 0.1 copy.171
  194.5 0.1 copy.140
  194.6 0.4 fusion.22
  195.0 0.3 fusion.69
  195.3 3.4 fusion.19
  198.7 1.8 copy.157
  200.6 2.1 reshape.105
  202.7 7.9 %multiply_reduce_fusion = (f32[1024]{0:T(1024)S(1)}, f32[1024,256]{1,0:T(8,128)}) fusion(bf16[1024,4096]{0,1:T(8,128)(2,1)} %fusion.3, bf16[4096,256]{1,0:T(8,128)(2,1)} %param.16, f32[1024,256]{1,0:T(8,128)} %reshape.105, f32[1024,256]{1,0:T(8,128)S(1)} %divide_multiply_fusion.1, f32[256]{0:T(256)S(1)} %mul.273), kind=kOutput, calls=%fused_computation.62 | convolution fusion | flops 2150366208 | bytes 13636608 | tf_op jit(solution)/shard_map/dot_general | solution.py:78
  210.7 19.9 %all_to_all.25 = f32[32,1,1024]{2,1,0:T(1,128)S(1)} all-to-all(f32[32,1,1024]{2,1,0:T(1,128)S(1)} %broadcast_in_dim.32), channel_id=1, replica_groups=mesh['seq'=8,'chan'=32] {'chan'}, dimensions={0} | all-to-all | bytes 262144 | tf_op jit(solution)/shard_map/all_to_all | solution.py:35
  230.7 2.2 multiply_convert_fusion
  233.0 2.5 copy.146
  235.5 41.0 %all_to_all.26 = bf16[256,32,128]{0,2,1:T(8,128)(2,1)S(1)} all-to-all(bf16[256,32,128]{0,2,1:T(8,128)(2,1)} %bitcast.101), channel_id=1, replica_groups=mesh['seq'=8,'chan'=32] {'chan'}, dimensions={1} | all-to-all | bytes 4194304 | tf_op jit(solution)/shard_map/all_to_all | solution.py:134
  276.5 2.9 copy.147
  279.4 50.9 %all-gather.10.cloned.1.call-done = bf16[1024,8192]{1,0:T(8,128)(2,1)} async-done(((bf16[1024,256]{1,0:T(8,128)(2,1)}), bf16[1024,8192]{1,0:T(8,128)(2,1)}) %all-gather.10.cloned.1.call-update) | async-done | bytes 16777232 | tf_op jit(solution)/shard_map/all_gather | solution.py:136
  330.2 11.8 %fusion.23 = bf16[1024,128]{1,0:T(8,128)(2,1)} fusion(bf16[1024,8192]{1,0:T(8,128)(2,1)} %all-gather.10.cloned.1.call-done, bf16[8192,128]{1,0:T(8,128)(2,1)} %bitcast.104, bf16[1024,128]{1,0:T(8,128)(2,1)S(1)} %copy-done.4), kind=kOutput, calls=%fused_computation.35 | convolution fusion | flops 2147876864 | bytes 19398656 | tf_op jit(solution)/shard_map/dot_general | solution.py:135
  (61 shorter events, 1.4 us)
Async XLA Ops:
  6.5 129.5 %copy-start = (bf16[4096,256]{1,0:T(8,128)(2,1)S(1)}, bf16[4096,256]{1,0:T(8,128)(2,1)}, u32[]{:S(2)}) copy-start(bf16[4096,256]{1,0:T(8,128)(2,1)} %param.17) | copy-start | bytes 6291460
  6.5 65.4 %all-gather.12.cloned.1.call-start = ((), (), s32[]{:S(2)}) async-start(), calls=%async_computation.4 | async-start | bytes 8650752 | tf_op jit(solution)/shard_map/all_gather | solution.py:73
  7.3 116.7 %all-gather.8.cloned.1.call-start = ((), (), s32[]{:S(2)}) async-start(), calls=%async_computation.2 | async-start | bytes 3244032 | tf_op jit(solution)/shard_map/all_gather | solution.py:84
  8.0 178.1 %all-gather.14.cloned.1.call-start = ((), (), s32[]{:S(2)}) async-start(), calls=%async_computation.5 | async-start | bytes 1179648 | tf_op jit(solution)/shard_map/all_gather | solution.py:21
  100.5 5.1 %copy-start.5 = (f32[4096]{0:T(1024)S(1)}, f32[4096]{0:T(1024)}, u32[]{:S(2)}) copy-start(f32[4096]{0:T(1024)} %param.15) | copy-start | bytes 49156
  114.9 20.6 %copy-start.7 = (f32[4]{0:T(128)S(1)}, f32[4]{0:T(128)}, u32[]{:S(2)}) copy-start(f32[4]{0:T(128)} %param.22) | copy-start | bytes 52
  131.9 3.2 copy-start.2
  131.9 17.8 %collective-permute-start.1 = (f32[3,256]{1,0:T(4,128)S(1)}, f32[3,256]{1,0:T(4,128)S(1)}, u32[]{:S(2)}, u32[]{:S(2)}) collective-permute-start(f32[3,256]{1,0:T(4,128)S(1)} %slice.92), channel_id=1, source_target_pairs={{0,32},{32,64},{64,96},{96,128},{128,160},{160,192},{192,224},{1,3... | collective-permute-start | bytes 9224 | tf_op jit(solution)/shard_map/ppermute | solution.py:16
  141.8 3.9 %collective-permute-start = (bf16[3,256]{1,0:T(4,128)(2,1)S(1)}, bf16[3,256]{1,0:T(4,128)(2,1)S(1)}, u32[]{:S(2)}, u32[]{:S(2)}) collective-permute-start(bf16[3,256]{1,0:T(4,128)(2,1)S(1)} %slice.161), channel_id=1, source_target_pairs={{0,32},{32,64},{64,96},{96,128},{128,160},{160,192},{192,224},{1,3... | collective-permute-start | bytes 4616 | tf_op jit(solution)/shard_map/ppermute | solution.py:16
  145.0 4.6 %slice-start = ((f32[1024,384]{1,0:T(8,128)}), f32[1024,256]{1,0:T(8,128)S(1)}, s32[]{:S(2)}) async-start(f32[1024,384]{1,0:T(8,128)} %copy-done.2), calls=%async_computation.6 | async-start | bytes 2097152 | tf_op jit(solution)/shard_map/slice | solution.py:87
  147.7 3.7 %copy-start.8 = (f32[4]{0:T(128)S(1)}, f32[4]{0:T(128)}, u32[]{:S(2)}) copy-start(f32[4]{0:T(128)} %param.23) | copy-start | bytes 52
  151.3 178.9 %all-gather.10.cloned.1.call-start = ((), (), s32[]{:S(2)}) async-start(), calls=%async_computation.3 | async-start | bytes 17301504 | tf_op jit(solution)/shard_map/all_gather | solution.py:136
  202.7 28.0 %copy-start.6 = (f32[256]{0:T(256)S(1)}, f32[256]{0:T(256)}, u32[]{:S(2)}) copy-start(f32[256]{0:T(256)} %param.24) | copy-start | bytes 3076
  202.7 30.3 %copy-start.3 = (bf16[256,4096]{1,0:T(8,128)(2,1)S(1)}, bf16[256,4096]{1,0:T(8,128)(2,1)}, u32[]{:S(2)}) copy-start(bf16[256,4096]{1,0:T(8,128)(2,1)} %param.25) | copy-start | bytes 6291460
  235.5 94.8 %copy-start.4 = (bf16[1024,128]{1,0:T(8,128)(2,1)S(1)}, bf16[1024,128]{1,0:T(8,128)(2,1)}, u32[]{:S(2)}) copy-start(bf16[1024,128]{1,0:T(8,128)(2,1)} %param.14) | copy-start | bytes 786436
  330.2 11.8 %copy-start.1 = (bf16[4096,256]{1,0:T(8,128)(2,1)S(1)}, bf16[4096,256]{1,0:T(8,128)(2,1)}, u32[]{:S(2)}) copy-start(bf16[4096,256]{1,0:T(8,128)(2,1)} %param.17) | copy-start | bytes 6291460
Sparse Core Ops, SparseCore 0:
  9.9 61.9 all-gather.11
  74.4 49.4 all-gather.7
  151.4 34.5 all-gather.13
  233.1 97.0 all-gather.9
